TPU v7x, 32 devices: a whole 2x2x4 slice. The times are simulated.
32 devices in a mesh: chan: 2 (over x), vis: 2 (over core), pix: 8 (over z, y).
Axes of the slice: x: 2, y: 2, z: 4, core: 2. Of those that a mesh axis runs over, the one named last changes fastest.
Arguments:
- response: bfloat16 [16384, 49152], P(('chan', 'vis'), 'pix'), parts along dimension 0, may hold values from -5 to 5
- vis_data: float32 [16384], P(('chan', 'vis')), parts along dimension 0, may hold values from -6 to 6
- baseline_of_row: int32 [8192], P('vis'), may hold values from 0 to 8191
- noise_class: int32 [8192], P('vis'), may hold values from 0 to 15
- baseline_weight: float32 [8192], replicated, may hold values from 0.25 to 4
- class_inv_var: float32 [32], P('chan'), parts along dimension 0, may hold values from 0.25 to 4
Outputs:
- sky_map: float32 [98304], P(('chan', 'pix')), parts along dimension 0
- psf: float32 [98304, 64], P(('chan', 'pix'), 'vis'), parts along dimension 0
There are 2 independent parts, one for each index of `chan`. A program takes and returns all parts, laid end to end along the dimension named above; an argument that names none is the same for every part. Nothing has to cross between parts.
Inputs may be any that keep to these rules, and one draw needn't show every extreme that they name: `baseline_of_row`: baseline index of each row.
All inputs are finite; a program needn't handle non-finite values.
Results may differ from a plain program's by a relative error of at most 0.0041.
Values may be sent and summed in bfloat16 or wider, within the bound.
No kernel may reach another device: no remote copies, remote signals or barrier semaphores. Data moves between devices by JAX's collectives and lax.ppermute only.
A program may use at most 128 MiB of HBM per device.

v0:
```python
import jax
import jax.numpy as jnp
from jax import lax
from jax.sharding import PartitionSpec as P

PANEL_DEV = 8


def shards(response, vis_data, baseline_of_row, noise_class, baseline_weight, class_inv_var):
    classes = lax.broadcasted_iota(jnp.int32, (1, class_inv_var.shape[0]), 1)
    class_weight = jnp.sum(
        jnp.where(noise_class[:, None] == classes, class_inv_var[None, :], jnp.float32(0.0)), axis=1
    )
    weight_row = jnp.take(baseline_weight, baseline_of_row) * class_weight
    own_panel = response[:, :PANEL_DEV]
    pix_rows = response.shape[1]
    piece_cols = lax.all_gather(own_panel, "pix", axis=1, tiled=True)
    operand = (weight_row[:, None] * piece_cols.astype(jnp.float32)).astype(jnp.bfloat16)
    plain_f = piece_cols.astype(jnp.float32)
    beam_part = jnp.concatenate(
        [
            lax.dot_general(
                response, operand, (((0,), (0,)), ((), ())), preferred_element_type=jnp.float32
            ),
            jnp.sum(weight_row[:, None] * plain_f * plain_f, axis=0)[None, :],
        ],
        axis=0,
    )
    weighted_vis = (weight_row * vis_data).astype(jnp.bfloat16)
    dirty_part = jnp.dot(weighted_vis, response, preferred_element_type=jnp.float32)
    norm_part = jnp.sum(weight_row[:, None] * jnp.square(response.astype(jnp.float32)), axis=0)
    col_share = beam_part.shape[1] // lax.axis_size("vis")
    beam_all, dirty_map, pixel_norm = lax.psum((beam_part, dirty_part, norm_part), "vis")
    beam_rows = lax.dynamic_slice_in_dim(beam_all, lax.axis_index("vis") * col_share, col_share, 1)
    panel_scale = beam_rows[pix_rows]
    beam_rows = beam_rows[:pix_rows]
    sky_map = dirty_map / jnp.sqrt(pixel_norm)
    psf = beam_rows / jnp.sqrt(pixel_norm[:, None] * panel_scale[None, :])
    return (sky_map, psf)


def solution(mesh):
    placed = (P(("chan", "vis"), "pix"), P(("chan", "vis")), P("vis"), P("vis"), P(), P("chan"))
    return jax.shard_map(
        shards,
        mesh=mesh,
        in_specs=placed,
        out_specs=(P(("chan", "pix")), P(("chan", "pix"), "vis")),
        check_vma=False,
    )
```

profile of v0, /device:TPU:0, one launch (start us, length us, event | category | flops | bytes accessed | tf_op | source)
XLA Modules:
  0.0 140.9 jit_solution(5494770655249392284)
XLA Ops:
  7.2 0.0 copy-start
  7.2 0.0 all-reduce.3.cloned.1.call-start
  7.2 0.7 fusion.2
  8.0 1.3 slice.9
  9.2 0.3 copy.14
  9.6 33.0 %all_gather.3 = bf16[4096,64]{0,1:T(8,128)(2,1)S(1)} all-gather(bf16[4096,8]{0,1:T(8,128)(2,1)S(1)} %copy.14), channel_id=1, replica_groups=mesh['chan'=2,'vis'=2,'pix'=8] {'pix'}, dimensions={1}, use_global_device_ids=true | all-gather | bytes 589824 | tf_op jit(solution)/shard_map/all_gather | solution.py:17
  42.6 0.0 copy-done
  42.6 23.0 %gather_fusion = f32[4096]{0:T(1024)S(1)} fusion(f32[8192]{0:T(1024)S(1)} %copy-done, s32[4096]{0:T(1024)S(1)} %fusion.2), kind=kCustom, calls=%fused_computation | custom fusion | bytes 49152 | tf_op jit(solution)/shard_map/jit(_take)/gather | solution.py:14
  65.6 0.9 select_reduce_fusion
  66.5 0.8 multiply_convert_fusion.2
  67.2 19.8 %convolution_bitcast_fusion = f32[6144,64]{0,1:T(8,128)S(1)} fusion(bf16[4096,6144]{1,0:T(8,128)(2,1)} %param.6, bf16[4096,64]{0,1:T(8,128)(2,1)S(1)} %all_gather.3, f32[4096]{0:T(1024)S(1)} %get-tuple-element.5), kind=kOutput, calls=%fused_computation.2 | convolution fusion | flops 3222011904 | bytes 52445184 | tf_op jit(solution)/shard_map/dot_general | solution.py:22
  87.1 0.2 fusion
  87.3 0.1 copy.13
  87.4 1.3 pad_maximum_fusion
  88.7 0.0 all-reduce.3.cloned.1.call-update
  88.7 19.3 %multiply_reduce_fusion = f32[6144]{0:T(1024)S(1)} fusion(bf16[4096,6144]{1,0:T(8,128)(2,1)} %param.6, f32[4096]{0:T(1024)S(1)} %get-tuple-element.5), kind=kLoop, calls=%fused_computation.1 | loop fusion | flops 100657152 | bytes 50372608 | tf_op jit(solution)/shard_map/reduce_sum | solution.py:31
  108.0 18.9 %fusion.3 = f32[1,6144]{1,0:T(1,128)S(1)} fusion(bf16[4096,1]{0,1:T(2,128)(2,1)S(1)} %reshape.26, bf16[4096,6144]{1,0:T(8,128)(2,1)} %param.6), kind=kOutput, calls=%fused_computation.17 | convolution fusion | flops 50331648 | bytes 50364416 | tf_op jit(solution)/shard_map/dot_general | solution.py:30
  126.9 3.5 %all-reduce = (f32[6144]{0:T(1024)S(1)}, f32[6144]{0:T(1024)S(1)}) all-reduce(f32[6144]{0:T(1024)S(1)} %bitcast.7, f32[6144]{0:T(1024)S(1)} %multiply_reduce_fusion), channel_id=1, replica_groups=mesh['chan'=2,'vis'=2,'pix'=8] {'vis'}, use_global_device_ids=true, to_apply=%region_1.2 | all-reduce | flops 12288 | bytes 98304 | tf_op jit(solution)/shard_map/psum | solution.py:33
  130.4 0.6 rsqrt_multiply_fusion
  131.1 0.0 all-reduce.3.cloned.1.call-done
  131.1 0.8 dynamic-slice_reduce_fusion
  131.9 2.2 %dynamic-slice_multiply_fusion = f32[6144,32]{0,1:T(8,128)} fusion(f32[6145,64]{0,1:T(8,128)} %all-reduce.3.cloned.1.call-done, s32[]{:T(128)S(6)} %select_n.21, f32[32]{0:T(128)S(1)} %dynamic-slice_reduce_fusion, f32[6144]{0:T(1024)S(1)} %get-tuple-element.3), kind=kLoop, calls=%fused_computation.7 | loop fusion | flops 393216 | bytes 1597572 | tf_op jit(solution)/shard_map/div | solution.py:38
  (1 shorter events, 0.0 us)
Async XLA Ops:
  7.2 35.4 %copy-start = (f32[8192]{0:T(1024)S(1)}, f32[8192]{0:T(1024)}, u32[]{:S(2)}) copy-start(f32[8192]{0:T(1024)} %param.10) | copy-start | bytes 98308
  7.2 123.9 %all-reduce.3.cloned.1.call-start = ((), (), s32[]{:S(2)}) async-start(), calls=%async_computation | async-start | bytes 3211264 | tf_op jit(solution)/shard_map/psum | solution.py:33
Sparse Core Ops, SparseCore 0:
  88.8 21.5 all-reduce.2
where the time goes:
time: 142 us; the launch traced here: 141 us
  matrix products  38.7 us (27%)
  blocking collectives  36.6 us (26%)
  other arithmetic  26 us (18%)
  local copies, waits for them, and re-layouts  25.6 us (18%)
  between operations  14.1 us (10%)
    all_gather x1, blocking collectives, shards(): piece_cols = lax.all_gather(own_panel, 'pix', axis=1, tiled=True)  33 us
    gather x1, local copies, waits for them, and re-layouts, shards(): weight_row = jnp.take(baseline_weight, baseline_of_row) * class_weight  23 us
    dot_general x1, matrix products, shards(): lax.dot_general(response, operand, (((0,), (0,)), ((), ())), preferred_el...  19.8 us
    reduce_sum x1, other arithmetic, shards(): jnp.sum(weight_row[:, None] * jnp.square(response.astype(jnp.float32)), a...  19.3 us
    dot_general x1, matrix products, shards(): jnp.dot(weighted_vis, response, preferred_element_type=jnp.float32)  18.9 us
    psum x1, blocking collectives, shards(): lax.psum((beam_part, dirty_part, norm_part), 'vis')  3.53 us
  transfers between devices with their start and end apart: 1, of which 0 were waited for; matrix products, arithmetic and copies ran while one was open for 28% of the time, Pallas kernels for 0%

commit v1 on v0

--- a/solution.py
+++ b/solution.py
@@ -14,7 +14,10 @@
     weight_row = jnp.take(baseline_weight, baseline_of_row) * class_weight
     own_panel = response[:, :PANEL_DEV]
     pix_rows = response.shape[1]
-    piece_cols = lax.all_gather(own_panel, "pix", axis=1, tiled=True)
+    piece_cols = jnp.concatenate(
+        lax.all_to_all(jnp.stack([own_panel for _ in range(lax.psum(1, "pix"))]), "pix", 0, 0),
+        axis=1,
+    )
     operand = (weight_row[:, None] * piece_cols.astype(jnp.float32)).astype(jnp.bfloat16)
     plain_f = piece_cols.astype(jnp.float32)
     beam_part = jnp.concatenate(

time: 142 us -> 117 us (0.82)
  blocking collectives: 36.6 us -> 3.53 us
  starting transfers between devices: 0.04 us -> 7.35 us
    all_gather x1 -> x0, blocking collectives: 33 us -> none  [shards(): piece_cols = lax.all_gather(own_panel, 'pix', axis=1, tiled=True)]
    all_to_all x0 -> x1, starting transfers between devices: none -> 7.31 us  [shards(): lax.all_to_all(jnp.stack([own_panel for _ in range(lax.psum(1, 'pix'))]),...]
  transfers between devices with their start and end apart: 1 -> 2, of which waited for: 0 -> 0; matrix products, arithmetic and copies ran while one was open for 28% -> 56% of each run, Pallas kernels for 0% -> 0%
where the time goes in v1:
time: 117 us
  matrix products  39.3 us (34%)
  local copies, waits for them, and re-layouts  26.4 us (23%)
  other arithmetic  25.9 us (22%)
  between operations  14.1 us (12%)
  starting transfers between devices  7.35 us (6%)
  blocking collectives  3.53 us (3%)
    gather x1, local copies, waits for them, and re-layouts, shards(): weight_row = jnp.take(baseline_weight, baseline_of_row) * class_weight  23 us
    dot_general x1, matrix products, shards(): lax.dot_general(response, operand, (((0,), (0,)), ((), ())), preferred_el...  19.8 us
    dot_general x1, matrix products, shards(): jnp.dot(weighted_vis, response, preferred_element_type=jnp.float32)  19.5 us
    reduce_sum x1, other arithmetic, shards(): jnp.sum(weight_row[:, None] * jnp.square(response.astype(jnp.float32)), a...  19.3 us
    all_to_all x1, starting transfers between devices, shards(): lax.all_to_all(jnp.stack([own_panel for _ in range(lax.psum(1, 'pix'))]),...  7.31 us
    psum x1, blocking collectives, shards(): lax.psum((beam_part, dirty_part, norm_part), 'vis')  3.53 us
  transfers between devices with their start and end apart: 2, of which 0 were waited for; matrix products, arithmetic and copies ran while one was open for 56% of the time, Pallas kernels for 0%

profile of v1, /device:TPU:0, one launch (start us, length us, event | category | flops | bytes accessed | tf_op | source)
XLA Modules:
  0.0 116.6 jit_solution(17258936268169019747)
XLA Ops:
  7.2 0.0 copy-start
  7.2 1.3 %slice.9 = bf16[4096,8]{1,0:T(8,128)(2,1)S(1)} slice(bf16[4096,6144]{1,0:T(8,128)(2,1)} %param.6), slice={[0:4096], [0:8]} | slice | bytes 131072 | tf_op jit(solution)/shard_map/slice | solution.py:15
  8.5 0.3 copy.11
  8.8 0.8 stack.2
  9.6 7.3 %all-to-all-start = ((bf16[8,4096,8]{1,2,0:T(8,128)(2,1)}), bf16[8,4096,8]{1,2,0:T(8,128)(2,1)S(1)}, u32[]{:S(2)}, u32[]{:S(2)}) async-start(bf16[8,4096,8]{1,2,0:T(8,128)(2,1)} %stack.2), calls=%async_computation | async-start | bytes 1048576 | tf_op jit(solution)/shard_map/all_to_all | solution.py:18
  16.9 0.0 all-reduce.3.cloned.1.call-start
  17.0 0.7 fusion.5
  17.7 0.0 copy-done
  17.7 23.0 %gather_fusion = f32[4096]{0:T(1024)S(1)} fusion(f32[8192]{0:T(1024)S(1)} %copy-done, s32[4096]{0:T(1024)S(1)} %fusion.5), kind=kCustom, calls=%fused_computation | custom fusion | bytes 49152 | tf_op jit(solution)/shard_map/jit(_take)/gather | solution.py:14
  40.7 0.9 select_reduce_fusion
  41.6 0.8 multiply_convert_fusion
  42.4 19.3 %multiply_reduce_fusion = f32[6144]{0:T(1024)S(1)} fusion(bf16[4096,6144]{1,0:T(8,128)(2,1)} %param.6, f32[4096]{0:T(1024)S(1)} %get-tuple-element.5), kind=kLoop, calls=%fused_computation.1 | loop fusion | flops 100657152 | bytes 50372608 | tf_op jit(solution)/shard_map/reduce_sum | solution.py:34
  61.7 0.0 all-to-all-done
  61.7 0.2 fusion.2
  61.9 0.1 broadcast_in_dim.34
  62.0 19.8 %convolution_bitcast_fusion = f32[6144,64]{0,1:T(8,128)S(1)} fusion(bf16[4096,6144]{1,0:T(8,128)(2,1)} %param.6, bf16[8,4096,8]{1,2,0:T(8,128)(2,1)S(1)} %all-to-all-done, f32[4096]{0:T(1024)S(1)} %get-tuple-element.5), kind=kOutput, calls=%fused_computation.2 | convolution fusion | flops 3222011904 | bytes 52445184 | tf_op jit(solution)/shard_map/dot_general | solution.py:25
  81.8 1.3 %pad_maximum_fusion = f32[6145,64]{0,1:T(8,128)} fusion(f32[1,64]{0,1:T(8,128)S(1)} %broadcast_in_dim.34, f32[6144,64]{0,1:T(8,128)S(1)} %convolution_bitcast_fusion), kind=kLoop, calls=%fused_computation.3 | loop fusion | flops 393280 | bytes 3146240 | tf_op jit(solution)/shard_map/concatenate | solution.py:23
  83.1 0.0 all-reduce.3.cloned.1.call-update
  83.1 19.5 %fusion.6 = f32[1,6144]{1,0:T(1,128)S(1)} fusion(bf16[4096,1]{0,1:T(2,128)(2,1)S(1)} %reshape.40, bf16[4096,6144]{1,0:T(8,128)(2,1)} %param.6), kind=kOutput, calls=%fused_computation.20 | convolution fusion | flops 50331648 | bytes 50364416 | tf_op jit(solution)/shard_map/dot_general | solution.py:33
  102.6 3.5 %all-reduce = (f32[6144]{0:T(1024)S(1)}, f32[6144]{0:T(1024)S(1)}) all-reduce(f32[6144]{0:T(1024)S(1)} %bitcast.20, f32[6144]{0:T(1024)S(1)} %multiply_reduce_fusion), channel_id=1, replica_groups=mesh['chan'=2,'vis'=2,'pix'=8] {'vis'}, use_global_device_ids=true, to_apply=%region_1.2 | all-reduce | flops 12288 | bytes 98304 | tf_op jit(solution)/shard_map/psum | solution.py:36
  106.1 0.6 rsqrt_multiply_fusion
  106.8 0.0 all-reduce.3.cloned.1.call-done
  106.8 0.8 dynamic-slice_reduce_fusion
  107.6 2.2 %dynamic-slice_multiply_fusion = f32[6144,32]{0,1:T(8,128)} fusion(f32[6145,64]{0,1:T(8,128)} %all-reduce.3.cloned.1.call-done, s32[]{:T(128)S(6)} %select_n.21, f32[32]{0:T(128)S(1)} %dynamic-slice_reduce_fusion, f32[6144]{0:T(1024)S(1)} %get-tuple-element.3), kind=kLoop, calls=%fused_computation.10 | loop fusion | flops 393216 | bytes 1597572 | tf_op jit(solution)/shard_map/div | solution.py:41
  (1 shorter events, 0.0 us)
Async XLA Ops:
  7.2 10.5 %copy-start = (f32[8192]{0:T(1024)S(1)}, f32[8192]{0:T(1024)}, u32[]{:S(2)}) copy-start(f32[8192]{0:T(1024)} %param.10) | copy-start | bytes 98308
  9.6 52.0 %all-to-all-start = ((bf16[8,4096,8]{1,2,0:T(8,128)(2,1)}), bf16[8,4096,8]{1,2,0:T(8,128)(2,1)S(1)}, u32[]{:S(2)}, u32[]{:S(2)}) async-start(bf16[8,4096,8]{1,2,0:T(8,128)(2,1)} %stack.2), calls=%async_computation | async-start | bytes 1048576 | tf_op jit(solution)/shard_map/all_to_all | solution.py:18
  16.9 89.8 %all-reduce.3.cloned.1.call-start = ((), (), s32[]{:S(2)}) async-start(), calls=%async_computation.1 | async-start | bytes 3211264 | tf_op jit(solution)/shard_map/psum | solution.py:36
Sparse Core Ops, SparseCore 0:
  83.2 21.7 all-reduce.2
